TPU v7x, 32 devices: a whole 2x2x4 slice. The times are simulated.
32 devices in a mesh: groups: 2 (over x), col: 16 (over z, y, core).
Axes of the slice: x: 2, y: 2, z: 4, core: 2. Of those that a mesh axis runs over, the one named last changes fastest.
Arguments:
- left: bfloat16 [256, 64, 32], P('col', 'groups'), parts along dimension 1, may hold values from -18 to 18
- right: bfloat16 [256, 2560, 32], P('col', 'groups'), parts along dimension 1, may hold values from -18 to 18
- out_weight: bfloat16 [1024, 128], replicated, may hold values from -0.1875 to 0.1875
- out_bias: float32 [128], replicated, may hold values from -3 to 3
Outputs:
- pair_update: bfloat16 [64, 1280, 128], P('groups', 'col'), parts along dimension 0
There are 2 independent parts, one for each index of `groups`. A program takes and returns all parts, laid end to end along the dimension named above; an argument that names none is the same for every part. Nothing has to cross between parts.
All inputs are finite; a program needn't handle non-finite values.
Results may differ from a plain program's by a relative error of at most 0.004.
Values may be sent and summed in bfloat16 or wider, within the bound.
A program may use at most 64 MiB of HBM per device.

v0:
```python
import jax
import jax.numpy as jnp
from jax import lax
from jax.sharding import PartitionSpec as P


def tile_update(left_rows, right_cols, out_weight, out_bias):
    seqs, count, width = left_rows.shape
    columns = right_cols.shape[1]
    outer = (
        jnp.einsum("sic,sje->ijce", left_rows, right_cols, preferred_element_type=jnp.float32)
        / seqs
    )
    flat = outer.astype(jnp.bfloat16).reshape(count * columns, width * width)
    update = jnp.dot(flat, out_weight, preferred_element_type=jnp.float32) + out_bias
    return update.astype(jnp.bfloat16).reshape(count, columns, out_weight.shape[1])


def rows_update(left_rows, right_cols, out_weight, out_bias):
    seqs, count, width = left_rows.shape
    blocks = jnp.transpose(left_rows.reshape(seqs, count // 8, 8, width), (1, 0, 2, 3))
    results = lax.map(lambda block: tile_update(block, right_cols, out_weight, out_bias), blocks)
    return results.reshape(count, right_cols.shape[1], out_weight.shape[1])


def on_device(left, right, out_weight, out_bias):
    left_part, right_cols = (
        lax.all_to_all(left, "col", split_axis=1, concat_axis=0, tiled=True),
        lax.all_to_all(right, "col", split_axis=1, concat_axis=0, tiled=True),
    )
    return rows_update(
        lax.all_gather(left_part, "col", axis=1, tiled=True), right_cols, out_weight, out_bias
    )


def solution(mesh):
    in_specs = (P("col", "groups", None), P("col", "groups", None), P(), P())
    out_specs = P("groups", "col", None)
    return jax.shard_map(
        on_device, mesh=mesh, in_specs=in_specs, out_specs=out_specs, check_vma=False
    )
```

profile of v0, /device:TPU:9, one launch (start us, length us, event | category | flops | bytes accessed | tf_op | source)
XLA Modules:
  0.0 118.3 jit_solution(4670310625103489706)
XLA Ops:
  1.7 6.6 %all-to-all-start = ((bf16[16,2,512]{2,1,0:T(2,128)(2,1)}), bf16[16,2,512]{2,1,0:T(2,128)(2,1)S(1)}, u32[]{:S(2)}, u32[]{:S(2)}) async-start(bf16[16,2,512]{2,1,0:T(2,128)(2,1)} %reshape.16), calls=%async_computation | async-start | bytes 65536 | tf_op jit(solution)/shard_map/all_to_all | solution.py:28
  8.3 6.9 %copy.16 = bf16[16,1280,32]{2,0,1:T(8,128)(2,1)} copy(bf16[16,1280,32]{1,2,0:T(8,128)(2,1)} %param.7) | data formatting | bytes 2621440 | tf_op args[1]
  15.2 8.3 %reshape.18 = bf16[16,2,20480]{2,1,0:T(2,128)(2,1)} reshape(bf16[1280,16,32]{2,1,0:T(8,128)(2,1)} %bitcast.49) | data formatting | bytes 2621440
  23.5 6.0 %all-to-all-start.1 = ((bf16[16,2,20480]{2,1,0:T(2,128)(2,1)}), bf16[16,2,20480]{2,1,0:T(2,128)(2,1)S(1)}, u32[]{:S(2)}, u32[]{:S(2)}) async-start(bf16[16,2,20480]{2,1,0:T(2,128)(2,1)} %reshape.18), calls=%async_computation.1 | async-start | bytes 2621440 | tf_op jit(solution)/shard_map/all_to_all | solution.py:29
  29.8 43.8 %all_gather.3 = bf16[256,32,32]{0,2,1:T(8,128)(2,1)} all-gather(bf16[256,2,32]{0,2,1:T(8,128)(2,1)S(1)} %copy.15), channel_id=1, replica_groups=mesh['groups'=2,'col'=16] {'col'}, dimensions={1}, use_global_device_ids=true | all-gather | bytes 557056 | tf_op jit(solution)/shard_map/all_gather | solution.py:32
  73.6 4.0 %reshape.19 = bf16[1280,16,32]{2,1,0:T(8,128)(2,1)} reshape(bf16[16,2,20480]{2,1,0:T(2,128)(2,1)S(1)} %all-to-all-done.1) | data formatting | bytes 2621440
  77.6 6.8 %copy.17 = bf16[16,16,80,32]{2,3,0,1:T(8,128)(2,1)S(1)} copy(bf16[16,16,80,32]{3,0,2,1:T(8,128)(2,1)} %bitcast.48) | data formatting | bytes 2621440 | tf_op jit(solution)/shard_map/all_to_all | solution.py:29
  84.4 1.6 %copy.18 = bf16[256,80,32]{0,1,2:T(8,128)(2,1)S(1)} copy(bf16[256,80,32]{1,2,0:T(8,128)(2,1)S(1)} %bitcast.51) | data formatting | bytes 2621440 | tf_op jit(solution)/shard_map/while | solution.py:22
  86.0 32.3 %while.10 = (s32[]{:T(128)}, bf16[4,8,80,128]{3,2,1,0:T(8,128)(2,1)}, bf16[4,256,8,32]{1,3,2,0:T(8,128)(2,1)}, bf16[256,80,32]{0,1,2:T(8,128)(2,1)S(1)}, bf16[10...) while((s32[]{:T(128)}, bf16[4,8,80,128]{3,2,1,0:T(8,128)(2,1)}, bf16[4,256,8,32]{1,3,2,0:T(8,128)(2,1)}, ...), condition=%wide.region_1.2_spmd, body=%wide.region_0.1_spmd.sunk | while | flops 504791040 | bytes 20547204 | solution.py:22
  87.1 1.6 %fusion.18 = bf16[8,80,32,32]{1,2,3,0:T(8,128)(2,1)S(1)} fusion(bf16[256,80,32]{0,1,2:T(8,128)(2,1)S(1)} %get-tuple-element.116, bf16[4,256,8,32]{1,3,2,0:T(8,128)(2,1)} %get-tuple-element.115, s32[]{:T(128)} %get-tuple-element.106), kind=kOutput, calls=%fused_computation.1.clone.1 | convolution fusion | flops 336855040 | bytes 2753024 | tf_op jit(solution)/shard_map/while/body/eval_jaxpr/sic,sje->ijce/dot_general | solution.py:11
  88.7 1.4 %copy.23 = bf16[8,80,32,32]{1,0,3,2:T(8,128)(2,1)S(1)} copy(bf16[8,80,32,32]{1,2,3,0:T(8,128)(2,1)S(1)} %fusion.18) | data formatting | bytes 2621440 | tf_op jit(solution)/shard_map/while/body/eval_jaxpr/convert_element_type | solution.py:14
  90.1 1.7 %reshape.21 = bf16[640,1024]{0,1:T(8,128)(2,1)S(1)} reshape(bf16[8,80,32,32]{1,0,3,2:T(8,128)(2,1)S(1)} %copy.23) | data formatting | bytes 2621440 | tf_op jit(solution)/shard_map/while/body/eval_jaxpr/reshape | solution.py:14
  91.8 1.6 %fusion.19 = bf16[640,128]{1,0:T(8,128)(2,1)S(1)} fusion(bf16[640,1024]{0,1:T(8,128)(2,1)S(1)} %reshape.21, bf16[1024,128]{1,0:T(8,128)(2,1)} %get-tuple-element.117, f32[128]{0:T(128)S(1)} %get-tuple-element.118), kind=kOutput, calls=%fused_computation.4.clone.1 | convolution fusion | flops 167936000 | bytes 1737216 | tf_op jit(solution)/shard_map/while/body/eval_jaxpr/dot_general | solution.py:15
  95.2 1.6 %fusion.18 = bf16[8,80,32,32]{1,2,3,0:T(8,128)(2,1)S(1)} fusion(bf16[256,80,32]{0,1,2:T(8,128)(2,1)S(1)} %get-tuple-element.116, bf16[4,256,8,32]{1,3,2,0:T(8,128)(2,1)} %get-tuple-element.115, s32[]{:T(128)} %get-tuple-element.106), kind=kOutput, calls=%fused_computation.1.clone.1 | convolution fusion | flops 336855040 | bytes 2753024 | tf_op jit(solution)/shard_map/while/body/eval_jaxpr/sic,sje->ijce/dot_general | solution.py:11
  96.8 1.4 %copy.23 = bf16[8,80,32,32]{1,0,3,2:T(8,128)(2,1)S(1)} copy(bf16[8,80,32,32]{1,2,3,0:T(8,128)(2,1)S(1)} %fusion.18) | data formatting | bytes 2621440 | tf_op jit(solution)/shard_map/while/body/eval_jaxpr/convert_element_type | solution.py:14
  98.2 1.7 %reshape.21 = bf16[640,1024]{0,1:T(8,128)(2,1)S(1)} reshape(bf16[8,80,32,32]{1,0,3,2:T(8,128)(2,1)S(1)} %copy.23) | data formatting | bytes 2621440 | tf_op jit(solution)/shard_map/while/body/eval_jaxpr/reshape | solution.py:14
  99.9 1.6 %fusion.19 = bf16[640,128]{1,0:T(8,128)(2,1)S(1)} fusion(bf16[640,1024]{0,1:T(8,128)(2,1)S(1)} %reshape.21, bf16[1024,128]{1,0:T(8,128)(2,1)} %get-tuple-element.117, f32[128]{0:T(128)S(1)} %get-tuple-element.118), kind=kOutput, calls=%fused_computation.4.clone.1 | convolution fusion | flops 167936000 | bytes 1737216 | tf_op jit(solution)/shard_map/while/body/eval_jaxpr/dot_general | solution.py:15
  103.2 1.6 %fusion.18 = bf16[8,80,32,32]{1,2,3,0:T(8,128)(2,1)S(1)} fusion(bf16[256,80,32]{0,1,2:T(8,128)(2,1)S(1)} %get-tuple-element.116, bf16[4,256,8,32]{1,3,2,0:T(8,128)(2,1)} %get-tuple-element.115, s32[]{:T(128)} %get-tuple-element.106), kind=kOutput, calls=%fused_computation.1.clone.1 | convolution fusion | flops 336855040 | bytes 2753024 | tf_op jit(solution)/shard_map/while/body/eval_jaxpr/sic,sje->ijce/dot_general | solution.py:11
  106.2 1.7 %reshape.21 = bf16[640,1024]{0,1:T(8,128)(2,1)S(1)} reshape(bf16[8,80,32,32]{1,0,3,2:T(8,128)(2,1)S(1)} %copy.23) | data formatting | bytes 2621440 | tf_op jit(solution)/shard_map/while/body/eval_jaxpr/reshape | solution.py:14
  108.0 1.6 %fusion.19 = bf16[640,128]{1,0:T(8,128)(2,1)S(1)} fusion(bf16[640,1024]{0,1:T(8,128)(2,1)S(1)} %reshape.21, bf16[1024,128]{1,0:T(8,128)(2,1)} %get-tuple-element.117, f32[128]{0:T(128)S(1)} %get-tuple-element.118), kind=kOutput, calls=%fused_computation.4.clone.1 | convolution fusion | flops 167936000 | bytes 1737216 | tf_op jit(solution)/shard_map/while/body/eval_jaxpr/dot_general | solution.py:15
  111.3 1.6 %fusion.18 = bf16[8,80,32,32]{1,2,3,0:T(8,128)(2,1)S(1)} fusion(bf16[256,80,32]{0,1,2:T(8,128)(2,1)S(1)} %get-tuple-element.116, bf16[4,256,8,32]{1,3,2,0:T(8,128)(2,1)} %get-tuple-element.115, s32[]{:T(128)} %get-tuple-element.106), kind=kOutput, calls=%fused_computation.1.clone.1 | convolution fusion | flops 336855040 | bytes 2753024 | tf_op jit(solution)/shard_map/while/body/eval_jaxpr/sic,sje->ijce/dot_general | solution.py:11
  113.0 1.4 %copy.23 = bf16[8,80,32,32]{1,0,3,2:T(8,128)(2,1)S(1)} copy(bf16[8,80,32,32]{1,2,3,0:T(8,128)(2,1)S(1)} %fusion.18) | data formatting | bytes 2621440 | tf_op jit(solution)/shard_map/while/body/eval_jaxpr/convert_element_type | solution.py:14
  114.3 1.7 %reshape.21 = bf16[640,1024]{0,1:T(8,128)(2,1)S(1)} reshape(bf16[8,80,32,32]{1,0,3,2:T(8,128)(2,1)S(1)} %copy.23) | data formatting | bytes 2621440 | tf_op jit(solution)/shard_map/while/body/eval_jaxpr/reshape | solution.py:14
  116.0 1.6 %fusion.19 = bf16[640,128]{1,0:T(8,128)(2,1)S(1)} fusion(bf16[640,1024]{0,1:T(8,128)(2,1)S(1)} %reshape.21, bf16[1024,128]{1,0:T(8,128)(2,1)} %get-tuple-element.117, f32[128]{0:T(128)S(1)} %get-tuple-element.118), kind=kOutput, calls=%fused_computation.4.clone.1 | convolution fusion | flops 167936000 | bytes 1737216 | tf_op jit(solution)/shard_map/while/body/eval_jaxpr/dot_general | solution.py:15
  (31 shorter events, 10.3 us)
Async XLA Ops:
  1.7 21.8 %all-to-all-start = ((bf16[16,2,512]{2,1,0:T(2,128)(2,1)}), bf16[16,2,512]{2,1,0:T(2,128)(2,1)S(1)}, u32[]{:S(2)}, u32[]{:S(2)}) async-start(bf16[16,2,512]{2,1,0:T(2,128)(2,1)} %reshape.16), calls=%async_computation | async-start | bytes 65536 | tf_op jit(solution)/shard_map/all_to_all | solution.py:28
  23.5 50.1 %all-to-all-start.1 = ((bf16[16,2,20480]{2,1,0:T(2,128)(2,1)}), bf16[16,2,20480]{2,1,0:T(2,128)(2,1)S(1)}, u32[]{:S(2)}, u32[]{:S(2)}) async-start(bf16[16,2,20480]{2,1,0:T(2,128)(2,1)} %reshape.18), calls=%async_computation.1 | async-start | bytes 2621440 | tf_op jit(solution)/shard_map/all_to_all | solution.py:29
  84.4 1.6 %copy-start.2 = (f32[128]{0:T(128)S(1)}, f32[128]{0:T(128)}, u32[]{:S(2)}) copy-start(f32[128]{0:T(128)} %param.9) | copy-start | bytes 1540
  86.0 1.1 copy-start
  91.8 2.3 %copy-start.1 = (bf16[256,80,32]{0,1,2:T(8,128)(2,1)S(1)}, bf16[256,80,32]{0,1,2:T(8,128)(2,1)}, u32[]{:S(2)}) copy-start(bf16[256,80,32]{0,1,2:T(8,128)(2,1)} %copy-done) | copy-start | bytes 3932164 | tf_op jit(solution)/shard_map/while
  94.1 1.1 copy-start
  99.9 2.3 %copy-start.1 = (bf16[256,80,32]{0,1,2:T(8,128)(2,1)S(1)}, bf16[256,80,32]{0,1,2:T(8,128)(2,1)}, u32[]{:S(2)}) copy-start(bf16[256,80,32]{0,1,2:T(8,128)(2,1)} %copy-done) | copy-start | bytes 3932164 | tf_op jit(solution)/shard_map/while
  102.2 1.1 copy-start
  107.9 2.3 %copy-start.1 = (bf16[256,80,32]{0,1,2:T(8,128)(2,1)S(1)}, bf16[256,80,32]{0,1,2:T(8,128)(2,1)}, u32[]{:S(2)}) copy-start(bf16[256,80,32]{0,1,2:T(8,128)(2,1)} %copy-done) | copy-start | bytes 3932164 | tf_op jit(solution)/shard_map/while
  110.2 1.1 copy-start
  116.0 2.3 %copy-start.1 = (bf16[256,80,32]{0,1,2:T(8,128)(2,1)S(1)}, bf16[256,80,32]{0,1,2:T(8,128)(2,1)}, u32[]{:S(2)}) copy-start(bf16[256,80,32]{0,1,2:T(8,128)(2,1)} %copy-done) | copy-start | bytes 3932164 | tf_op jit(solution)/shard_map/while
where the time goes:
time: 119 us; the launch traced here: 118 us
  local copies, waits for them, and re-layouts  48.7 us (41%)
  blocking collectives  43.8 us (37%)
  matrix products  12.9 us (11%)
  starting transfers between devices  12.6 us (11%)
    all_gather x1, blocking collectives, on_device(): lax.all_gather(left_part, 'col', axis=1, tiled=True)  43.8 us
    unnamed x8, local copies, waits for them, and re-layouts  21.1 us
    reshape x4, local copies, waits for them, and re-layouts, tile_update(): flat = outer.astype(jnp.bfloat16).reshape(count * columns, width * width)  6.79 us
    all_to_all x1, local copies, waits for them, and re-layouts, on_device(): lax.all_to_all(right, 'col', split_axis=1, concat_axis=0, tiled=True)  6.76 us
    all_to_all x1, starting transfers between devices, on_device(): lax.all_to_all(left, 'col', split_axis=1, concat_axis=0, tiled=True)  6.58 us
    dot_general x4, matrix products, tile_update(): jnp.einsum('sic,sje->ijce', left_rows, right_cols, preferred_element_type...  6.53 us
    dot_general x4, matrix products, tile_update(): jnp.dot(flat, out_weight, preferred_element_type=jnp.float32) + out_bias  6.39 us
    all_to_all x1, starting transfers between devices, on_device(): lax.all_to_all(right, 'col', split_axis=1, concat_axis=0, tiled=True)  6.02 us
  transfers between devices with their start and end apart: 2, of which 0 were waited for; matrix products, arithmetic and copies ran while one was open for 13% of the time, Pallas kernels for 0%

commit v1 on v0

v1 whole, which is shorter than its diff:
```python
import functools

import jax
import jax.numpy as jnp
from jax import lax
from jax.experimental import pallas as pl
from jax.experimental.pallas import tpu as pltpu
from jax.sharding import PartitionSpec as P

MESH = pl.DeviceIdType.MESH
LANES = 128
TILE = 16


def flip_kernel(x_ref, o_ref):
    o_ref[...] = x_ref[...].T


def flip(x):
    rows, columns = x.shape
    step = 2 * LANES
    return pl.pallas_call(
        flip_kernel,
        grid=(columns // step,),
        in_specs=[pl.BlockSpec((rows, step), lambda g: (0, g))],
        out_specs=pl.BlockSpec((step, rows), lambda g: (g, 0)),
        out_shape=jax.ShapeDtypeStruct((columns, rows), x.dtype),
    )(x)


def swap_matrix(first, minor, start, rows, columns):
    row = lax.broadcasted_iota(jnp.int32, (rows, columns), 0) + start
    column = lax.broadcasted_iota(jnp.int32, (rows, columns), 1)
    shift = first.bit_length() - 1
    wanted = (row & (first - 1)) * minor + (row >> shift)
    return jnp.where(column == wanted, 1.0, 0.0).astype(jnp.bfloat16)


def kernel(
    n, width, cols, rows, right_ref, left_ref, weight_ref, bias_ref, out_ref,
    rbuf, lbuf, rwide, lturn, wturn, flat,
    rsend, rrecv, lsend, lrecv, fsend, own,
):
    me = lax.axis_index("col")
    mate = me + 1 - 2 * lax.rem(me, 2)
    half = n // 2
    pair = out_ref.shape[2]
    local = left_ref.shape[0]
    seqs = n * local

    def rcopy(k):
        to = lax.rem(me + k, n)
        start = pl.multiple_of(to * cols, TILE)
        return pltpu.make_async_remote_copy(
            src_ref=right_ref.at[pl.ds(start, cols)],
            dst_ref=rbuf.at[me],
            send_sem=rsend.at[k],
            recv_sem=rrecv.at[me],
            device_id={"col": to},
            device_id_type=MESH,
        )

    def lcopy(src, slot, to, send):
        return pltpu.make_async_remote_copy(
            src_ref=src,
            dst_ref=lbuf.at[slot],
            send_sem=send,
            recv_sem=lrecv.at[slot],
            device_id={"col": to},
            device_id_type=MESH,
        )

    barrier = pltpu.get_barrier_semaphore()
    for k in range(1, n):
        pl.semaphore_signal(
            barrier, inc=1, device_id={"col": lax.rem(me + k, n)}, device_id_type=MESH
        )
    pl.semaphore_wait(barrier, n - 1)

    sends = [lcopy(left_ref, me, mate, lsend.at[0])]
    for k in range(1, half):
        sends.append(lcopy(left_ref, me, lax.rem(me + 2 * k, n), lsend.at[k]))
    for k in range(1, n):
        sends.append(rcopy(k))
    for copy in sends:
        copy.start()
    mine = pltpu.make_async_copy(
        right_ref.at[pl.ds(pl.multiple_of(me * cols, TILE), cols)], rbuf.at[me], own.at[0]
    )
    mine.start()
    mine_left = pltpu.make_async_copy(left_ref, lbuf.at[me], own.at[1])
    mine_left.start()

    rwide[...] = jnp.zeros_like(rwide)
    channels = width * width
    for start in range(0, channels, LANES):
        chosen = swap_matrix(width, width, start, LANES, channels)
        block = jnp.dot(chosen, weight_ref[...], preferred_element_type=jnp.float32)
        wturn[:, start : start + LANES] = block.T.astype(jnp.bfloat16)
    swap = swap_matrix(TILE, width, 0, TILE * width, TILE * width)

    forwards = []
    for k in range(1, half):
        slot = lax.rem(me + n - 2 * k, n)
        lcopy(left_ref, slot, mate, lsend.at[k]).wait_recv()
        forward = lcopy(lbuf.at[slot], slot, mate, fsend.at[k])
        forward.start()
        forwards.append(forward)
    lcopy(left_ref, mate, mate, lsend.at[0]).wait_recv()
    for k in range(1, half):
        slot = lax.rem(mate + n - 2 * k, n)
        lcopy(left_ref, slot, mate, lsend.at[k]).wait_recv()
    mine_left.wait()
    per = TILE // local
    for group in range(seqs // TILE):
        parts = [lbuf[group * per + p] for p in range(per)]
        if per > 1:
            parts = [part.astype(jnp.float32) for part in parts]
            block = jnp.concatenate(parts, axis=0).astype(jnp.bfloat16)
        else:
            block = parts[0]
        lturn[group * TILE : (group + 1) * TILE, :] = block

    mine.wait()
    for k in range(1, n):
        slot = lax.rem(me + n - k, n)
        pltpu.make_async_remote_copy(
            src_ref=right_ref.at[pl.ds(0, cols)],
            dst_ref=rbuf.at[slot],
            send_sem=rsend.at[k],
            recv_sem=rrecv.at[slot],
            device_id={"col": slot},
            device_id_type=MESH,
        ).wait_recv()
    for group in range(seqs // TILE):
        parts = [rbuf[group * per + p] for p in range(per)]
        block = parts[0] if per == 1 else jnp.concatenate(parts, axis=1)
        turned = lax.dot_general(
            swap, block, (((1,), (1,)), ((), ())), preferred_element_type=jnp.float32
        ).astype(jnp.bfloat16)
        for e in range(width):
            rwide[group * TILE : (group + 1) * TILE, e * LANES : e * LANES + cols] = turned[
                e * TILE : (e + 1) * TILE
            ]

    count = flat.shape[0] * 2
    for base in range(0, rows, count):
        turned = lturn[:, base * width : (base + count) * width].T

        def outer(step, carry):
            lanes = pl.ds(pl.multiple_of(step * 2 * LANES, 2 * LANES), 2 * LANES)
            product = jnp.dot(
                turned, rwide[:, lanes], preferred_element_type=jnp.float32
            ).astype(jnp.bfloat16)
            for half_e in range(2):
                at = pl.ds(pl.multiple_of((step * 2 + half_e) * width, width), width)
                for i in range(count):
                    side = (i % 2) * LANES
                    flat[i // 2, at, side : side + LANES] = product[
                        i * width : (i + 1) * width, half_e * LANES : (half_e + 1) * LANES
                    ]
            return carry

        lax.fori_loop(0, width // 2, outer, 0)

        def project(step, carry):
            update = jnp.dot(wturn[...], flat[step], preferred_element_type=jnp.float32).T
            update = update * (1.0 / seqs) + bias_ref[...]
            update = update.astype(out_ref.dtype)
            out_ref[base + 2 * step] = update[:cols]
            out_ref[base + 2 * step + 1] = update[LANES : LANES + cols]
            return carry

        lax.fori_loop(0, count // 2, project, 0)

    for copy in sends + forwards:
        copy.wait_send()


def on_device(n, left, right, out_weight, out_bias):
    local, rows, width = left.shape
    cols = right.shape[1] // n
    pair = out_weight.shape[1]
    seqs = local * n
    wide = jnp.transpose(right, (0, 2, 1)).reshape(local * width, right.shape[1])
    turned = flip(wide)
    rows_step = min(rows, 32)
    vmem = pl.BlockSpec(memory_space=pltpu.VMEM)
    dma = pltpu.SemaphoreType.DMA
    return pl.pallas_call(
        functools.partial(kernel, n, width, cols, rows),
        out_shape=jax.ShapeDtypeStruct((rows, cols, pair), jnp.bfloat16),
        in_specs=[vmem] * 4,
        out_specs=vmem,
        scratch_shapes=[
            pltpu.VMEM((n, cols, local * width), jnp.bfloat16),
            pltpu.VMEM((n, local, rows * width), jnp.bfloat16),
            pltpu.VMEM((seqs, width * LANES), jnp.bfloat16),
            pltpu.VMEM((seqs, rows * width), jnp.bfloat16),
            pltpu.VMEM((pair, width * width), jnp.bfloat16),
            pltpu.VMEM((rows_step // 2, width * width, 2 * LANES), jnp.bfloat16),
            dma((n,)), dma((n,)), dma((n // 2,)), dma((n,)), dma((n // 2,)), dma((2,)),
        ],
        compiler_params=pltpu.CompilerParams(
            collective_id=0, has_side_effects=True, vmem_limit_bytes=60 * 1024 * 1024
        ),
    )(turned, left.reshape(local, rows * width), out_weight, out_bias.reshape(1, pair))


def solution(mesh):
    return jax.shard_map(
        functools.partial(on_device, mesh.shape["col"]),
        mesh=mesh,
        in_specs=(P("col", "groups", None), P("col", "groups", None), P(), P()),
        out_specs=P("groups", "col", None),
        check_vma=False,
    )
```

time: 119 us -> 62.3 us (0.52)
  the two profiles are of different devices: /device:TPU:9 before, /device:TPU:29 now
where the time goes in v1:
time: 62.3 us; the launch traced here: 61.8 us
  Pallas kernels  58.1 us (93%)
  local copies, waits for them, and re-layouts  3.66 us (6%)
    pallas_call x1, Pallas kernels, on_device(): pl.pallas_call(functools.partial(kernel, n, width, cols, rows), out_shape...  53.8 us
    pallas_call x1, Pallas kernels, flip(): pl.pallas_call(flip_kernel, grid=(columns // step,), in_specs=[pl.BlockSp...  4.25 us
    unnamed x1, local copies, waits for them, and re-layouts  1.97 us
    reshape x1, local copies, waits for them, and re-layouts, on_device(): left.reshape(local, rows * width)  1.69 us

profile of v1, /device:TPU:29, one launch (start us, length us, event | category | flops | bytes accessed | tf_op | source)
XLA Modules:
  0.0 61.8 jit_solution(6950802201590016223)
XLA Ops:
  0.0 1.7 %reshape.10.left_ref = bf16[16,1024]{1,0:T(8,128)(2,1)} reshape(bf16[16,32,32]{2,1,0:T(8,128)(2,1)} %param.4) | data formatting | bytes 65536 | tf_op jit(solution)/shard_map/reshape | solution.py:207
  1.7 4.2 %shard_map.46.right_ref = bf16[1280,512]{1,0:T(8,128)(2,1)} custom-call(bf16[512,1280]{1,0:T(8,128)(2,1)} %bitcast.4), custom_call_target="tpu_custom_call" | custom-call | tf_op jit(solution)/shard_map/pallas_call | solution.py:22
  5.9 53.8 %shard_map.47 = bf16[32,80,128]{2,1,0:T(8,128)(2,1)} custom-call(bf16[1280,512]{1,0:T(8,128)(2,1)} %shard_map.46.right_ref, bf16[16,1024]{1,0:T(8,128)(2,1)} %reshape.10.left_ref, bf16[1024,128]{1,0:T(8,128)(2,1)} %weight_ref.1, f32[1,128]{1,0:T(1,128)} %bitcast.5), custom_call_target="tpu_custom_call" | custom-call | tf_op jit(solution)/shard_map/pallas_call | solution.py:190
  59.8 2.0 %copy.6 = bf16[32,80,128]{2,1,0:T(8,128)(2,1)} copy(bf16[32,80,128]{2,1,0:T(8,128)(2,1)} %shard_map.47) | data formatting | bytes 1310720

commit v2 on v1

v2 whole, which is shorter than its diff:
```python
import functools

import jax
import jax.numpy as jnp
from jax import lax
from jax.experimental import pallas as pl
from jax.experimental.pallas import tpu as pltpu
from jax.sharding import PartitionSpec as P

MESH = pl.DeviceIdType.MESH
LANES = 128
TILE = 16
GROUP = 4


def flip_kernel(x_ref, o_ref):
    chunks, _, lanes = o_ref.shape
    local, width, step = x_ref.shape
    part = width // chunks
    for h in range(chunks):
        piece = x_ref[:, h * part : (h + 1) * part, :]
        o_ref[h] = piece.reshape(lanes, step).T


def flip(x, chunks):
    local, width, columns = x.shape
    step = 2 * LANES
    lanes = local * width // chunks
    return pl.pallas_call(
        flip_kernel,
        grid=(columns // step,),
        in_specs=[pl.BlockSpec((local, width, step), lambda g: (0, 0, g))],
        out_specs=pl.BlockSpec((chunks, step, lanes), lambda g: (0, g, 0)),
        out_shape=jax.ShapeDtypeStruct((chunks, columns, lanes), x.dtype),
    )(x)


def swap_matrix(first, minor, start, rows, columns):
    row = lax.broadcasted_iota(jnp.int32, (rows, columns), 0) + start
    column = lax.broadcasted_iota(jnp.int32, (rows, columns), 1)
    shift = first.bit_length() - 1
    wanted = (row & (first - 1)) * minor + (row >> shift)
    return jnp.where(column == wanted, 1.0, 0.0).astype(jnp.bfloat16)


def kernel(
    n, width, cols, rows, chunks, right_ref, left_ref, weight_ref, bias_ref, out_ref,
    rbuf, lbuf, rwide, lturn, wturn, flat, partial,
    rsend, rrecv, lsend, lrecv, fsend, own,
):
    me = lax.axis_index("col")
    place = lax.rem(me, GROUP)
    mates = [me - place + lax.rem(place + j, GROUP) for j in range(1, GROUP)]
    hops = n // GROUP
    local = left_ref.shape[0]
    seqs = n * local
    part = width // chunks

    def rcopy(h, k):
        to = lax.rem(me + k, n)
        start = pl.multiple_of(to * cols, TILE)
        return pltpu.make_async_remote_copy(
            src_ref=right_ref.at[h, pl.ds(start, cols)],
            dst_ref=rbuf.at[h, me],
            send_sem=rsend.at[h, k],
            recv_sem=rrecv.at[h, me],
            device_id={"col": to},
            device_id_type=MESH,
        )

    def lcopy(src, slot, to, send):
        return pltpu.make_async_remote_copy(
            src_ref=src,
            dst_ref=lbuf.at[slot],
            send_sem=send,
            recv_sem=lrecv.at[slot],
            device_id={"col": to},
            device_id_type=MESH,
        )

    barrier = pltpu.get_barrier_semaphore()
    for k in range(1, n):
        pl.semaphore_signal(
            barrier, inc=1, device_id={"col": lax.rem(me + k, n)}, device_id_type=MESH
        )
    pl.semaphore_wait(barrier, n - 1)

    sends = []
    for k in range(1, hops):
        sends.append(lcopy(left_ref, me, lax.rem(me + GROUP * k, n), lsend.at[k]))
    for j, mate in enumerate(mates):
        sends.append(lcopy(left_ref, me, mate, fsend.at[0, j]))
    for h in range(chunks):
        for k in range(1, n):
            sends.append(rcopy(h, k))
    for copy in sends:
        copy.start()
    mine = []
    for h in range(chunks):
        block = right_ref.at[h, pl.ds(pl.multiple_of(me * cols, TILE), cols)]
        mine.append(pltpu.make_async_copy(block, rbuf.at[h, me], own.at[h]))
        mine[h].start()
    mine_left = pltpu.make_async_copy(left_ref, lbuf.at[me], own.at[chunks])
    mine_left.start()

    rwide[...] = jnp.zeros_like(rwide)
    channels = width * width
    for start in range(0, channels, LANES):
        chosen = swap_matrix(width, width, start, LANES, channels)
        block = jnp.dot(chosen, weight_ref[...], preferred_element_type=jnp.float32)
        wturn[:, start : start + LANES] = block.T.astype(jnp.bfloat16)
    swap = swap_matrix(TILE, part, 0, TILE * part, TILE * part)

    forwards = []
    for k in range(1, hops):
        slot = lax.rem(me + n - GROUP * k, n)
        lcopy(left_ref, slot, mates[0], lsend.at[k]).wait_recv()
        for j, mate in enumerate(mates):
            forward = lcopy(lbuf.at[slot], slot, mate, fsend.at[k, j])
            forward.start()
            forwards.append(forward)
    for k in range(hops):
        for j, mate in enumerate(mates):
            slot = lax.rem(mate + n - GROUP * k, n)
            lcopy(left_ref, slot, mate, fsend.at[k, j]).wait_recv()
    mine_left.wait()
    per = TILE // local
    blocks = []
    for group in range(seqs // TILE):
        parts = [lbuf[group * per + p] for p in range(per)]
        if per > 1:
            parts = [piece.astype(jnp.float32) for piece in parts]
            blocks.append(jnp.concatenate(parts, axis=0).astype(jnp.bfloat16))
        else:
            blocks.append(parts[0])
    lturn[...] = jnp.concatenate(blocks, axis=0).T

    def turn(h, start, block):
        turned = lax.dot_general(
            swap, block, (((1,), (1,)), ((), ())), preferred_element_type=jnp.float32
        ).astype(jnp.bfloat16)
        for e in range(part):
            at = (h * part + e) * LANES
            rwide[pl.ds(start, TILE), at : at + cols] = turned[e * TILE : (e + 1) * TILE]

    def arrive(h):
        def one(k, carry):
            slot = lax.rem(me + n - k, n)
            pltpu.make_async_remote_copy(
                src_ref=right_ref.at[h, pl.ds(0, cols)],
                dst_ref=rbuf.at[h, slot],
                send_sem=rsend.at[h, k],
                recv_sem=rrecv.at[h, slot],
                device_id={"col": slot},
                device_id_type=MESH,
            ).wait_recv()
            if per == 1:
                turn(h, pl.multiple_of(slot * TILE, TILE), rbuf[h, slot])
            return carry

        mine[h].wait()
        if per == 1:
            turn(h, pl.multiple_of(me * TILE, TILE), rbuf[h, me])
        lax.fori_loop(1, n, one, 0)
        if per > 1:
            for group in range(seqs // TILE):
                parts = [rbuf[h, group * per + p] for p in range(per)]
                turn(h, group * TILE, jnp.concatenate(parts, axis=1))

    count = flat.shape[0] * 2

    def multiply(base, h):
        def outer(step, carry):
            lanes = pl.ds(pl.multiple_of(step * 2 * LANES, 2 * LANES), 2 * LANES)
            product = jnp.dot(
                lturn[base * width : (base + count) * width, :],
                rwide[:, lanes],
                preferred_element_type=jnp.float32,
            ).astype(jnp.bfloat16)
            for side_e in range(2):
                at = pl.ds(pl.multiple_of((step * 2 + side_e) * width, width), width)
                for i in range(count):
                    side = (i % 2) * LANES
                    flat[i // 2, at, side : side + LANES] = product[
                        i * width : (i + 1) * width, side_e * LANES : (side_e + 1) * LANES
                    ]
            return carry

        lax.fori_loop(h * part // 2, (h + 1) * part // 2, outer, 0)

    deep = part * width
    early = rows == count and chunks > 1

    def project_early(step, carry):
        partial[step] = jnp.dot(
            wturn[:, : channels - deep],
            flat[step, : channels - deep],
            preferred_element_type=jnp.float32,
        )
        return carry

    for h in range(chunks):
        arrive(h)
        if rows == count:
            multiply(0, h)
        if early and h == chunks - 2:
            lax.fori_loop(0, count // 2, project_early, 0)

    skip = channels - deep if early else 0
    for base in range(0, rows, count):
        if rows != count:
            for h in range(chunks):
                multiply(base, h)

        def project(step, carry):
            update = jnp.dot(
                wturn[:, skip:], flat[step, skip:], preferred_element_type=jnp.float32
            )
            if early:
                update = update + partial[step]
            update = update.T * (1.0 / seqs) + bias_ref[...]
            update = update.astype(out_ref.dtype)
            out_ref[base + 2 * step] = update[:cols]
            out_ref[base + 2 * step + 1] = update[LANES : LANES + cols]
            return carry

        lax.fori_loop(0, count // 2, project, 0)

    for copy in sends + forwards:
        copy.wait_send()


def on_device(n, left, right, out_weight, out_bias):
    local, rows, width = left.shape
    cols = right.shape[1] // n
    pair = out_weight.shape[1]
    seqs = local * n
    chunks = 2 if local * width % (4 * LANES) == 0 else 1
    turned = flip(jnp.transpose(right, (0, 2, 1)), chunks)
    rows_step = min(rows, 32)
    vmem = pl.BlockSpec(memory_space=pltpu.VMEM)
    dma = pltpu.SemaphoreType.DMA
    return pl.pallas_call(
        functools.partial(kernel, n, width, cols, rows, chunks),
        out_shape=jax.ShapeDtypeStruct((rows, cols, pair), jnp.bfloat16),
        in_specs=[vmem] * 4,
        out_specs=vmem,
        scratch_shapes=[
            pltpu.VMEM((chunks, n, cols, local * width // chunks), jnp.bfloat16),
            pltpu.VMEM((n, local, rows * width), jnp.bfloat16),
            pltpu.VMEM((seqs, width * LANES), jnp.bfloat16),
            pltpu.VMEM((rows * width, seqs), jnp.bfloat16),
            pltpu.VMEM((pair, width * width), jnp.bfloat16),
            pltpu.VMEM((rows_step // 2, width * width, 2 * LANES), jnp.bfloat16),
            pltpu.VMEM((rows_step // 2, pair, 2 * LANES), jnp.float32),
            dma((chunks, n)), dma((chunks, n)),
            dma((n // GROUP,)), dma((n,)), dma((n // GROUP, GROUP)), dma((chunks + 1,)),
        ],
        compiler_params=pltpu.CompilerParams(
            collective_id=0, has_side_effects=True, vmem_limit_bytes=60 * 1024 * 1024
        ),
    )(turned, left.reshape(local, rows * width), out_weight, out_bias.reshape(1, pair))


def solution(mesh):
    return jax.shard_map(
        functools.partial(on_device, mesh.shape["col"]),
        mesh=mesh,
        in_specs=(P("col", "groups", None), P("col", "groups", None), P(), P()),
        out_specs=P("groups", "col", None),
        check_vma=False,
    )
```

time: 62.3 us -> 57 us (0.915)
  Pallas kernels: 58.1 us -> 53 us
    pallas_call x1, Pallas kernels: 53.8 us -> 48.8 us  [on_device(): pl.pallas_call(functools.partial(kernel, n, width, cols, rows, chunks), o...]
where the time goes in v2:
time: 57 us; the launch traced here: 56.7 us
  Pallas kernels  53 us (93%)
  local copies, waits for them, and re-layouts  3.66 us (6%)
    pallas_call x1, Pallas kernels, on_device(): pl.pallas_call(functools.partial(kernel, n, width, cols, rows, chunks), o...  48.8 us
    pallas_call x1, Pallas kernels, flip(): pl.pallas_call(flip_kernel, grid=(columns // step,), in_specs=[pl.BlockSp...  4.26 us
    unnamed x1, local copies, waits for them, and re-layouts  1.97 us
    reshape x1, local copies, waits for them, and re-layouts, on_device(): left.reshape(local, rows * width)  1.69 us

profile of v2, /device:TPU:29, one launch (start us, length us, event | category | flops | bytes accessed | tf_op | source)
XLA Modules:
  0.0 56.7 jit_solution(11666921909689670872)
XLA Ops:
  0.0 1.7 %reshape.6.left_ref = bf16[16,1024]{1,0:T(8,128)(2,1)} reshape(bf16[16,32,32]{2,1,0:T(8,128)(2,1)} %param.4) | data formatting | bytes 65536 | tf_op jit(solution)/shard_map/reshape | solution.py:262
  1.7 4.3 %shard_map.46.right_ref = bf16[2,1280,256]{2,1,0:T(8,128)(2,1)} custom-call(bf16[16,32,1280]{2,1,0:T(8,128)(2,1)} %bitcast.2), custom_call_target="tpu_custom_call" | custom-call | tf_op jit(solution)/shard_map/pallas_call | solution.py:29
  6.0 48.8 %shard_map.47 = bf16[32,80,128]{2,1,0:T(8,128)(2,1)} custom-call(bf16[2,1280,256]{2,1,0:T(8,128)(2,1)} %shard_map.46.right_ref, bf16[16,1024]{1,0:T(8,128)(2,1)} %reshape.6.left_ref, bf16[1024,128]{1,0:T(8,128)(2,1)} %weight_ref.1, f32[1,128]{1,0:T(1,128)} %bitcast.3), custom_call_target="tpu_custom_call" | custom-call | tf_op jit(solution)/shard_map/pallas_call | solution.py:243
  54.7 2.0 %copy.6 = bf16[32,80,128]{2,1,0:T(8,128)(2,1)} copy(bf16[32,80,128]{2,1,0:T(8,128)(2,1)} %shard_map.47) | data formatting | bytes 1310720

commit v3 on v2

--- a/solution.py
+++ b/solution.py
@@ -13,26 +13,13 @@
 GROUP = 4
 
 
-def flip_kernel(x_ref, o_ref):
-    chunks, _, lanes = o_ref.shape
-    local, width, step = x_ref.shape
-    part = width // chunks
-    for h in range(chunks):
-        piece = x_ref[:, h * part : (h + 1) * part, :]
-        o_ref[h] = piece.reshape(lanes, step).T
-
-
-def flip(x, chunks):
-    local, width, columns = x.shape
+def flip(x_ref, o_ref, h):
+    chunks, columns, lanes = o_ref.shape
+    part = x_ref.shape[1] // chunks
     step = 2 * LANES
-    lanes = local * width // chunks
-    return pl.pallas_call(
-        flip_kernel,
-        grid=(columns // step,),
-        in_specs=[pl.BlockSpec((local, width, step), lambda g: (0, 0, g))],
-        out_specs=pl.BlockSpec((chunks, step, lanes), lambda g: (0, g, 0)),
-        out_shape=jax.ShapeDtypeStruct((chunks, columns, lanes), x.dtype),
-    )(x)
+    for start in range(0, columns, step):
+        piece = x_ref[:, h * part : (h + 1) * part, start : start + step]
+        o_ref[h, start : start + step] = piece.reshape(lanes, step).T
 
 
 def swap_matrix(first, minor, start, rows, columns):
@@ -44,8 +31,8 @@
 
 
 def kernel(
-    n, width, cols, rows, chunks, right_ref, left_ref, weight_ref, bias_ref, out_ref,
-    rbuf, lbuf, rwide, lturn, wturn, flat, partial,
+    n, width, cols, rows, chunks, given_ref, left_ref, weight_ref, bias_ref, out_ref,
+    right_ref, rbuf, lbuf, rwide, lturn, wturn, flat, partial,
     rsend, rrecv, lsend, lrecv, fsend, own,
 ):
     me = lax.axis_index("col")
@@ -83,6 +70,7 @@
         pl.semaphore_signal(
             barrier, inc=1, device_id={"col": lax.rem(me + k, n)}, device_id_type=MESH
         )
+    flip(given_ref, right_ref, 0)
     pl.semaphore_wait(barrier, n - 1)
 
     sends = []
@@ -90,16 +78,12 @@
         sends.append(lcopy(left_ref, me, lax.rem(me + GROUP * k, n), lsend.at[k]))
     for j, mate in enumerate(mates):
         sends.append(lcopy(left_ref, me, mate, fsend.at[0, j]))
-    for h in range(chunks):
-        for k in range(1, n):
-            sends.append(rcopy(h, k))
+    for k in range(1, n):
+        sends.append(rcopy(0, k))
     for copy in sends:
         copy.start()
-    mine = []
-    for h in range(chunks):
-        block = right_ref.at[h, pl.ds(pl.multiple_of(me * cols, TILE), cols)]
-        mine.append(pltpu.make_async_copy(block, rbuf.at[h, me], own.at[h]))
-        mine[h].start()
+    for h in range(1, chunks):
+        flip(given_ref, right_ref, h)
     mine_left = pltpu.make_async_copy(left_ref, lbuf.at[me], own.at[chunks])
     mine_left.start()
 
@@ -109,6 +93,16 @@
         chosen = swap_matrix(width, width, start, LANES, channels)
         block = jnp.dot(chosen, weight_ref[...], preferred_element_type=jnp.float32)
         wturn[:, start : start + LANES] = block.T.astype(jnp.bfloat16)
+    for h in range(1, chunks):
+        later = [rcopy(h, k) for k in range(1, n)]
+        for copy in later:
+            copy.start()
+        sends += later
+    mine = []
+    for h in range(chunks):
+        block = right_ref.at[h, pl.ds(pl.multiple_of(me * cols, TILE), cols)]
+        mine.append(pltpu.make_async_copy(block, rbuf.at[h, me], own.at[h]))
+        mine[h].start()
     swap = swap_matrix(TILE, part, 0, TILE * part, TILE * part)
 
     forwards = []
@@ -236,7 +230,6 @@
     pair = out_weight.shape[1]
     seqs = local * n
     chunks = 2 if local * width % (4 * LANES) == 0 else 1
-    turned = flip(jnp.transpose(right, (0, 2, 1)), chunks)
     rows_step = min(rows, 32)
     vmem = pl.BlockSpec(memory_space=pltpu.VMEM)
     dma = pltpu.SemaphoreType.DMA
@@ -246,6 +239,7 @@
         in_specs=[vmem] * 4,
         out_specs=vmem,
         scratch_shapes=[
+            pltpu.VMEM((chunks, right.shape[1], local * width // chunks), jnp.bfloat16),
             pltpu.VMEM((chunks, n, cols, local * width // chunks), jnp.bfloat16),
             pltpu.VMEM((n, local, rows * width), jnp.bfloat16),
             pltpu.VMEM((seqs, width * LANES), jnp.bfloat16),
@@ -259,7 +253,7 @@
         compiler_params=pltpu.CompilerParams(
             collective_id=0, has_side_effects=True, vmem_limit_bytes=60 * 1024 * 1024
         ),
-    )(turned, left.reshape(local, rows * width), out_weight, out_bias.reshape(1, pair))
+    )(jnp.transpose(right, (0, 2, 1)), left.reshape(local, rows * width), out_weight, out_bias.reshape(1, pair))
 
 
 def solution(mesh):

time: 57 us -> 52.6 us (0.923)
  Pallas kernels: 53 us -> 48.7 us
    pallas_call x1 -> x0, Pallas kernels: 4.26 us -> none  [flip(): pl.pallas_call(flip_kernel, grid=(columns // step,), in_specs=[pl.BlockSp...]
where the time goes in v3:
time: 52.6 us; the launch traced here: 52.4 us
  Pallas kernels  48.7 us (93%)
  local copies, waits for them, and re-layouts  3.66 us (7%)
    pallas_call x1, Pallas kernels, on_device(): pl.pallas_call(functools.partial(kernel, n, width, cols, rows, chunks), o...  48.7 us
    unnamed x1, local copies, waits for them, and re-layouts  1.97 us
    reshape x1, local copies, waits for them, and re-layouts, on_device(): left.reshape(local, rows * width)  1.69 us

profile of v3, /device:TPU:29, one launch (start us, length us, event | category | flops | bytes accessed | tf_op | source)
XLA Modules:
  0.0 52.4 jit_solution(10184115690670508297)
XLA Ops:
  0.0 1.7 %reshape.6.left_ref = bf16[16,1024]{1,0:T(8,128)(2,1)} reshape(bf16[16,32,32]{2,1,0:T(8,128)(2,1)} %param.4) | data formatting | bytes 65536 | tf_op jit(solution)/shard_map/reshape | solution.py:256
  1.7 48.7 %shard_map.46 = bf16[32,80,128]{2,1,0:T(8,128)(2,1)} custom-call(bf16[16,32,1280]{2,1,0:T(8,128)(2,1)} %bitcast.2, bf16[16,1024]{1,0:T(8,128)(2,1)} %reshape.6.left_ref, bf16[1024,128]{1,0:T(8,128)(2,1)} %weight_ref.1, f32[1,128]{1,0:T(1,128)} %bitcast.3), custom_call_target="tpu_custom_call" | custom-call | tf_op jit(solution)/shard_map/pallas_call | solution.py:236
  50.4 2.0 %copy.6 = bf16[32,80,128]{2,1,0:T(8,128)(2,1)} copy(bf16[32,80,128]{2,1,0:T(8,128)(2,1)} %shard_map.46) | data formatting | bytes 1310720
